TPU v7x, 32 devices: a whole 2x2x4 slice. The times are simulated.
32 devices in a mesh: rows: 8 (over z, y), rep: 4 (over x, core).
Axes of the slice: x: 2, y: 2, z: 4, core: 2. Of those that a mesh axis runs over, the one named last changes fastest.
Arguments:
- embeddings: bfloat16 [2048, 1024], P('rows', 'rep'), may hold values from -6 to 6
- coarse_ids: int32 [2048], P('rows'), may hold values from 0 to 255
- fine_ids: int32 [2048], P('rows'), may hold values from 0 to 65535, as said below
- pq_codes: int32 [2048, 64], P('rows', 'rep'), may hold values from 0 to 255
- old_coarse: float32 [256, 1024], P(None, 'rep'), may hold values from -3 to 3
- old_fine: float32 [65536, 1024], P('rows', 'rep'), may hold values from -3 to 3
- old_codebook: float32 [256, 1024], P('rows', 'rep'), may hold values from -3 to 3
Outputs:
- new_coarse: float32 [256, 1024], P(None, 'rep')
- new_fine: float32 [65536, 1024], P('rows', 'rep')
- residual: bfloat16 [2048, 1024], P('rows', 'rep')
- new_codebook: float32 [256, 1024], P('rows', 'rep')
- row_error: float32 [2048], P('rows')
Inputs may be any that keep to these rules, and one draw needn't show every extreme that they name: `fine_ids`: within each aligned block of 256 rows, at most 128 ids lie in any one range o * 8192 to (o + 1) * 8192 - 1, and in every block some range holds exactly 128 of them.
All inputs are finite; a program needn't handle non-finite values.
Results may differ from a plain program's by a relative error of at most 0.0049.
Values may be sent and summed in bfloat16 or wider, within the bound.
No kernel may reach another device: no remote copies, remote signals or barrier semaphores. Data moves between devices by JAX's collectives and lax.ppermute only.
A program may use at most 64 MiB of HBM per device.

v0:
```python
import functools
import math

import jax
import jax.numpy as jnp
from jax import lax
from jax.experimental import pallas as pl
from jax.experimental.pallas import tpu as pltpu
from jax.sharding import PartitionSpec as P


def update_means(sums, counts, fallback):
    return jnp.where(counts[:, None] > 0, sums / jnp.maximum(counts, 1.0)[:, None], fallback)


def exchange_shards(embeddings, coarse_ids, fine_ids, pq_codes, old_coarse, old_fine, old_codebook):
    owner_rows = lax.axis_size("rows")
    row_total, width_dev = embeddings.shape
    coarse_total = old_coarse.shape[0]
    coarse_hot = coarse_ids[None, :] == jnp.arange(coarse_total, dtype=jnp.int32)[:, None]
    coarse_sum = jnp.dot(
        coarse_hot.astype(jnp.bfloat16), embeddings, preferred_element_type=jnp.float32
    )
    coarse_count = jnp.sum(coarse_hot, axis=1).astype(jnp.float32)
    coarse_sum, coarse_count = lax.psum((coarse_sum, coarse_count), "rows")
    new_coarse = update_means(coarse_sum, coarse_count, old_coarse)
    coarse_residual = (
        embeddings.astype(jnp.float32) - jnp.take(new_coarse, coarse_ids, axis=0)
    ).astype(jnp.bfloat16)
    fine_dev = old_fine.shape[0]
    capacity = 4 * row_total // owner_rows
    slot_total = owner_rows * capacity
    owner_ids = fine_ids // fine_dev
    local_ids = fine_ids % fine_dev
    owner_hot = (owner_ids[:, None] == jnp.arange(owner_rows, dtype=jnp.int32)[None, :]).astype(
        jnp.int32
    )
    rank_in = jnp.sum(jnp.cumsum(owner_hot, axis=0) * owner_hot, axis=1) - 1
    slot_of_row = owner_ids * capacity + rank_in
    row_of_slot = (
        jnp.full((slot_total,), row_total, jnp.int32)
        .at[slot_of_row]
        .set(jnp.arange(row_total, dtype=jnp.int32))
    )
    send_rows = jnp.take(coarse_residual, row_of_slot, axis=0, mode="fill", fill_value=0).reshape(
        owner_rows, capacity, width_dev
    )
    send_ids = (
        jnp.full((slot_total,), -1, jnp.int32)
        .at[slot_of_row]
        .set(local_ids)
        .reshape(owner_rows, capacity)
    )
    recv_rows, recv_ids = (
        lax.all_to_all(send_rows, "rows", split_axis=0, concat_axis=0, tiled=True),
        lax.all_to_all(send_ids, "rows", split_axis=0, concat_axis=0, tiled=True),
    )
    rows_flat = recv_rows.reshape(slot_total, width_dev)
    ids_flat = recv_ids.reshape(slot_total)
    block_size = math.gcd(slot_total, 2048)
    fine_range = jnp.arange(fine_dev, dtype=jnp.int32)

    def fine_step(running, pieces):
        sums, counts = running
        block_rows, block_ids = pieces
        one_hot = block_ids[None, :] == fine_range[:, None]
        sums = sums + jnp.dot(
            one_hot.astype(jnp.bfloat16), block_rows, preferred_element_type=jnp.float32
        )
        counts = counts + jnp.sum(one_hot, axis=1).astype(jnp.float32)
        return ((sums, counts), None)

    start_fine = (
        jnp.zeros((fine_dev, width_dev), jnp.float32),
        jnp.zeros((fine_dev,), jnp.float32),
    )
    (fine_sum, fine_count), _ = lax.scan(
        fine_step,
        start_fine,
        (
            rows_flat.reshape(slot_total // block_size, block_size, width_dev),
            ids_flat.reshape(slot_total // block_size, block_size),
        ),
    )
    new_fine = update_means(fine_sum, fine_count, old_fine)
    safe_ids = jnp.maximum(ids_flat, 0)
    at_owner = (rows_flat.astype(jnp.float32) - jnp.take(new_fine, safe_ids, axis=0)).astype(
        jnp.bfloat16
    )
    returned = lax.all_to_all(
        at_owner.reshape(owner_rows, capacity, width_dev),
        "rows",
        split_axis=0,
        concat_axis=0,
        tiled=True,
    ).reshape(slot_total, width_dev)
    residual = jnp.take(returned, slot_of_row, axis=0)
    sub_dev = pq_codes.shape[1]
    sub_width = width_dev // sub_dev
    share_codes = old_codebook.shape[0]
    book_rows = share_codes * owner_rows
    code_block = math.gcd(row_total, 512)
    code_range = jnp.arange(book_rows, dtype=jnp.int32)

    def code_step(running, pieces):
        sums, counts = running
        block_rows, block_codes = pieces
        one_hot = block_codes.T[:, None, :] == code_range[None, :, None]
        split_rows = block_rows.reshape(code_block, sub_dev, sub_width)
        sums = sums + jnp.einsum(
            "mkn,nmd->kmd",
            one_hot.astype(jnp.bfloat16),
            split_rows,
            preferred_element_type=jnp.float32,
        )
        counts = counts + jnp.sum(one_hot, axis=2).T.astype(jnp.float32)
        return ((sums, counts), None)

    start_code = (
        jnp.zeros((book_rows, sub_dev, sub_width), jnp.float32),
        jnp.zeros((book_rows, sub_dev), jnp.float32),
    )
    (code_sum, code_count), _ = lax.scan(
        code_step,
        start_code,
        (
            residual.reshape(row_total // code_block, code_block, width_dev),
            pq_codes.reshape(row_total // code_block, code_block, sub_dev),
        ),
    )
    code_sum = code_sum.reshape(book_rows, width_dev)
    code_sum, code_count = lax.psum((code_sum, code_count), "rows")
    column_count = jnp.repeat(code_count, sub_width, axis=1)
    averages = code_sum / jnp.maximum(column_count, 1.0)
    first_code = lax.axis_index("rows") * share_codes
    own_count = lax.dynamic_slice_in_dim(column_count, first_code, share_codes, 0)
    own_average = lax.dynamic_slice_in_dim(averages, first_code, share_codes, 0)
    new_codebook = jnp.where(own_count > 0, own_average, old_codebook)
    book_view = averages.reshape(book_rows, sub_dev, sub_width)
    rebuilt = book_view[pq_codes, jnp.arange(sub_dev, dtype=jnp.int32)[None, :]].reshape(
        row_total, width_dev
    )
    differ = residual.astype(jnp.float32) - rebuilt
    partial_error = jnp.sum(differ * differ, axis=1)
    row_error = lax.psum(partial_error, "rep") / (width_dev * lax.axis_size("rep"))
    return (new_coarse, new_fine, residual, new_codebook, row_error)


PACK = 16
NN = (((1,), (0,)), ((), ()))
NT = (((1,), (1,)), ((), ()))
GROUP = 8


def mm(left, right, dims):
    return lax.dot_general(left, right, dims, preferred_element_type=jnp.float32)


def thirds(value):
    high = value.astype(jnp.bfloat16)
    rest = value - high.astype(jnp.float32)
    middle = rest.astype(jnp.bfloat16)
    low = (rest - middle.astype(jnp.float32)).astype(jnp.bfloat16)
    return jnp.concatenate([high, middle, low], axis=0)


def whole(pieces):
    size = pieces.shape[0] // 3
    return (pieces[:size] + pieces[size : 2 * size]) + pieces[2 * size :]


def pack_kernel(emb_ref, coarse_ref, fine_ref, codes_ref, out_ref):
    width = emb_ref.shape[1]
    rows = emb_ref.shape[0]
    out_ref[:width] = emb_ref[...].T
    fine = fine_ref[...]
    place = lax.broadcasted_iota(jnp.int32, (PACK, rows), 0)
    ids = jnp.where(
        place == 0,
        1,
        jnp.where(
            place == 1, coarse_ref[...], jnp.where(place == 2, fine >> 8, jnp.where(place == 3, fine & 255, 0))
        ),
    )
    out_ref[width : width + PACK] = ids.astype(jnp.float32).astype(jnp.bfloat16)
    out_ref[width + PACK :] = codes_ref[...].astype(jnp.float32).astype(jnp.bfloat16)


def stage_kernel(coarse_ref, book_ref, coarse_out, book_out):
    coarse_out[...] = coarse_ref[...]
    book_out[...] = book_ref[...]


def steps_kernel(blocks, *refs):
    parts = refs[:blocks]
    (old_coarse_ref, old_book_ref, old_fine_ref) = refs[blocks : blocks + 3]
    (new_coarse_ref, new_fine_ref, residual_ref, new_book_ref, error_ref) = refs[blocks + 3 : blocks + 8]
    (table, feat, crs, mean_rows, res, books, counts, columns, slots_v, slots_s) = refs[
        blocks + 8 : blocks + 18
    ]
    (in_sem, out_sem, list_sem) = refs[blocks + 18 :]
    coarse_total, width = old_coarse_ref.shape
    share = old_book_ref.shape[0]
    fine_dev = old_fine_ref.shape[0]
    rows = parts[0].shape[1]
    total = rows * blocks
    sub_dev = parts[0].shape[0] - width - PACK
    sub_width = width // sub_dev
    code_total = share * blocks
    me = lax.axis_index("rows")

    load = pltpu.make_async_copy(old_fine_ref, table.at[:fine_dev], in_sem)
    load.start()
    for b in range(blocks):
        feat[:, b * rows : (b + 1) * rows] = parts[b][...]

    steps = slots_s.shape[0] // blocks
    slot_max = steps * GROUP
    digits = [
        jnp.concatenate([parts[b][width + 2 + d : width + 3 + d].astype(jnp.float32) for b in range(blocks)], axis=0)
        for d in range(2)
    ]
    ids8 = (digits[0] * 256.0 + digits[1]).astype(jnp.int32)
    local8 = ids8 - me * fine_dev
    mine = jnp.logical_and(local8 >= 0, local8 < fine_dev)
    mine_f = jnp.where(mine, 1.0, 0.0)
    earlier = lax.broadcasted_iota(jnp.int32, (rows, rows), 0) < lax.broadcasted_iota(jnp.int32, (rows, rows), 1)
    rank = mm(mine_f.astype(jnp.bfloat16), jnp.where(earlier, 1.0, 0.0).astype(jnp.bfloat16), NN)
    rank = jnp.where(mine, rank.astype(jnp.int32), -1)
    local8 = jnp.where(mine, local8, 0)
    lane = lax.broadcasted_iota(jnp.int32, (1, rows), 1)
    place = lax.broadcasted_iota(jnp.int32, (slot_max, rows), 0)
    slot_at = (place % steps) * GROUP + place // steps
    list_lane = lax.broadcasted_iota(jnp.int32, (steps, slots_s.shape[1]), 1)
    for b in range(blocks):
        pick = jnp.where(slot_at == rank[b : b + 1], 1.0, 0.0).astype(jnp.bfloat16)
        mine_b = local8[b : b + 1]
        values = jnp.concatenate(
            [(mine_b >> 8).astype(jnp.float32), (mine_b & 255).astype(jnp.float32), lane.astype(jnp.float32)]
            + [jnp.zeros((5, rows), jnp.float32)],
            axis=0,
        ).astype(jnp.bfloat16)
        got = mm(pick, values, NT)
        amount = jnp.sum(mine_f[b : b + 1], axis=1, keepdims=True).astype(jnp.int32)
        goal = (got[:, 0:1] * 256.0 + got[:, 1:2]).astype(jnp.int32)
        goal = jnp.where(slot_at[:, :1] < amount, goal, fine_dev)
        source = got[:, 2:3].astype(jnp.int32) + b * rows
        listed = jnp.broadcast_to((amount + GROUP - 1) // GROUP, list_lane.shape)
        for k in range(GROUP):
            part = slice(k * steps, (k + 1) * steps)
            listed = jnp.where(list_lane == k, goal[part], listed)
            listed = jnp.where(list_lane == GROUP + k, source[part], listed)
        slots_v[b * steps : (b + 1) * steps, :] = listed
    listing = pltpu.make_async_copy(slots_v, slots_s, list_sem)
    listing.start()

    digit_col = feat[width : width + PACK, :].astype(jnp.float32).T
    code_lane = lax.broadcasted_iota(jnp.int32, (1, coarse_total), 1).astype(jnp.float32)
    hot = jnp.where(digit_col[:, 1:2] == code_lane, 1.0, 0.0).astype(jnp.bfloat16)
    sums = mm(feat[: width + PACK, :], hot, NN)
    count = sums[width : width + 1]
    average = sums[:width] / jnp.maximum(count, 1.0)
    filled = jnp.broadcast_to(count, (width, coarse_total)).T > 0
    new_coarse_ref[...] = jnp.where(filled, average.T, old_coarse_ref[...])
    coarse_at = lax.broadcasted_iota(jnp.int32, (coarse_total, rows), 0).astype(jnp.float32)
    pieces = thirds(average)
    ones = jnp.where(lax.broadcasted_iota(jnp.int32, (PACK, rows), 0) == 0, 1.0, 0.0).astype(jnp.bfloat16)
    for b in range(blocks):
        cols = slice(b * rows, (b + 1) * rows)
        code_row = feat[width + 1 : width + 2, cols].astype(jnp.float32)
        hot = jnp.where(coarse_at == code_row, 1.0, 0.0).astype(jnp.bfloat16)
        near = whole(mm(pieces, hot, NN))
        crs[:width, cols] = (feat[:width, cols].astype(jnp.float32) - near).astype(jnp.bfloat16)
        crs[width:, cols] = ones

    id_row = feat[width + 2 : width + 3, :].astype(jnp.float32) * 256.0 + feat[width + 3 : width + 4, :].astype(
        jnp.float32
    )
    id_col = jnp.broadcast_to(digit_col[:, 2:3] * 256.0 + digit_col[:, 3:4], (total, 128))
    for b in range(blocks):
        cols = slice(b * rows, (b + 1) * rows)
        same = jnp.concatenate(
            [
                jnp.where(id_col == id_row[:, at : at + 128], 1.0, 0.0).astype(jnp.bfloat16)
                for at in range(b * rows, (b + 1) * rows, 128)
            ],
            axis=1,
        )
        fine = mm(crs[...], same, NN)
        mean = fine[:width] / fine[width : width + 1]
        res[:, cols] = (crs[:width, cols].astype(jnp.float32) - mean).astype(jnp.bfloat16)
        mean_rows[cols, 0, :] = mean.T
    residual_ref[...] = res[:, :rows].astype(jnp.float32).T.astype(jnp.bfloat16)

    listing.wait()
    load.wait()
    for b in range(blocks):

        def put(i, carry):
            means = [mean_rows[slots_s[i, GROUP + k]] for k in range(GROUP)]
            for k in range(GROUP):
                table[pl.ds(slots_s[i, k], 1), :] = means[k]
            return carry

        lax.fori_loop(b * steps, b * steps + slots_s[b * steps, 2 * GROUP], put, 0)
    store = pltpu.make_async_copy(table.at[:fine_dev], new_fine_ref, out_sem)
    store.start()

    columns[...] = feat[width + PACK :, :].astype(jnp.float32).T
    code_at = lax.broadcasted_iota(jnp.int32, (code_total, rows), 0).astype(jnp.float32)
    code_lane = lax.broadcasted_iota(jnp.int32, (1, code_total), 1).astype(jnp.float32)
    ones_all = jnp.where(lax.broadcasted_iota(jnp.int32, (PACK, total), 0) == 0, 1.0, 0.0).astype(jnp.bfloat16)
    error = jnp.zeros((sub_width, rows), jnp.float32)
    for m in range(sub_dev):
        band = slice(m * sub_width, (m + 1) * sub_width)
        hot_m = jnp.where(columns[:, m : m + 1] == code_lane, 1.0, 0.0).astype(jnp.bfloat16)
        sums = mm(jnp.concatenate([res[band, :], ones_all], axis=0), hot_m, NN)
        count = sums[sub_width : sub_width + 1]
        average = sums[:sub_width] / jnp.maximum(count, 1.0)
        books[band, :] = average
        counts[band, :] = jnp.broadcast_to(count, (sub_width, code_total))
        row = feat[width + PACK + m : width + PACK + m + 1, :rows].astype(jnp.float32)
        near = whole(mm(thirds(average), jnp.where(code_at == row, 1.0, 0.0).astype(jnp.bfloat16), NN))
        differ = res[band, :rows].astype(jnp.float32) - near
        error = error + differ * differ
    error_ref[...] = jnp.sum(error, axis=0, keepdims=True)
    books[...] = books[...].T
    counts[...] = counts[...].T
    own = pl.ds(pl.multiple_of(me * share, share), share)
    new_book_ref[...] = jnp.where(counts[own, :] > 0, books[own, :], old_book_ref[...])
    store.wait()


def gather_blocks(block, count):
    def hop(value, pairs):
        return lax.ppermute(value, "rows", pairs)

    half = count // 2
    near = [block]
    for k in range(1, half):
        near.append(hop(block, [(i, (i + 2 * k) % count) for i in range(count)]))
    far = [hop(value, [(i, i ^ 1) for i in range(count)]) for value in near]
    return near + far


def gathered_shards(embeddings, coarse_ids, fine_ids, pq_codes, old_coarse, old_fine, old_codebook):
    blocks = lax.axis_size("rows")
    rows, width = embeddings.shape
    coarse_total = old_coarse.shape[0]
    fine_dev = old_fine.shape[0]
    sub_dev = pq_codes.shape[1]
    share = old_codebook.shape[0]
    code_total = share * blocks
    total = rows * blocks
    slot_max = max(4 * rows // blocks, 1)
    height = width + PACK + sub_dev
    block = pl.pallas_call(
        pack_kernel,
        out_shape=pltpu.VMEM((height, rows), jnp.bfloat16),
    )(embeddings, coarse_ids.reshape(1, rows), fine_ids.reshape(1, rows), pq_codes.T)
    parts = gather_blocks(block, blocks)
    vmem = pl.BlockSpec(memory_space=pltpu.VMEM)
    coarse_near, book_near = pl.pallas_call(
        stage_kernel,
        out_shape=(pltpu.VMEM(old_coarse.shape, jnp.float32), pltpu.VMEM(old_codebook.shape, jnp.float32)),
        in_specs=[vmem] * 2,
        cost_estimate=pl.CostEstimate(flops=10**6, bytes_accessed=10**6, transcendentals=0),
    )(old_coarse, old_codebook)
    hbm = pl.BlockSpec(memory_space=pltpu.HBM)
    new_coarse, new_fine, residual, new_book, error = pl.pallas_call(
        functools.partial(steps_kernel, blocks),
        out_shape=(
            jax.ShapeDtypeStruct(old_coarse.shape, jnp.float32),
            jax.ShapeDtypeStruct(old_fine.shape, jnp.float32),
            jax.ShapeDtypeStruct(embeddings.shape, jnp.bfloat16),
            jax.ShapeDtypeStruct(old_codebook.shape, jnp.float32),
            jax.ShapeDtypeStruct((1, rows), jnp.float32),
        ),
        in_specs=[vmem] * (blocks + 2) + [hbm],
        out_specs=(vmem, hbm, vmem, vmem, vmem),
        scratch_shapes=[
            pltpu.VMEM((fine_dev + GROUP, width), jnp.float32),
            pltpu.VMEM((height, total), jnp.bfloat16),
            pltpu.VMEM((width + PACK, total), jnp.bfloat16),
            pltpu.VMEM((total, 1, width), jnp.float32),
            pltpu.VMEM((width, total), jnp.bfloat16),
            pltpu.VMEM((width, code_total), jnp.float32),
            pltpu.VMEM((width, code_total), jnp.float32),
            pltpu.VMEM((total, sub_dev), jnp.float32),
            pltpu.VMEM((blocks * slot_max // GROUP, 128), jnp.int32),
            pltpu.SMEM((blocks * slot_max // GROUP, 128), jnp.int32),
        ]
        + [pltpu.SemaphoreType.DMA] * 3,
        compiler_params=pltpu.CompilerParams(vmem_limit_bytes=48 * 2**20),
    )(*parts, coarse_near, book_near, old_fine)
    row_error = jnp.sum(lax.all_gather(error, "rep", axis=0, tiled=True), axis=0) / (width * lax.axis_size("rep"))
    return (new_coarse, new_fine, residual, new_book, row_error)


def fits(sizes):
    rows, width, blocks, fine_dev, sub_dev, code_total, coarse_total, fine_total = sizes
    digits = 256
    return (
        blocks % 2 == 0
        and rows * blocks <= fine_dev
        and rows % 128 == 0
        and rows <= digits
        and coarse_total <= digits
        and code_total <= digits
        and fine_total <= digits * digits
        and width == code_total
        and width // sub_dev == PACK
        and sub_dev % PACK == 0
        and (4 * rows // blocks) % 128 == 0
    )


def shards(*args):
    embeddings, _, _, pq_codes, old_coarse, old_fine, old_codebook = args
    blocks = lax.axis_size("rows")
    rows, width = embeddings.shape
    fine_dev = old_fine.shape[0]
    sizes = (
        rows,
        width,
        blocks,
        fine_dev,
        pq_codes.shape[1],
        old_codebook.shape[0] * blocks,
        old_coarse.shape[0],
        fine_dev * blocks,
    )
    return gathered_shards(*args) if fits(sizes) else exchange_shards(*args)


def solution(mesh):
    placed = (
        P("rows", "rep"),
        P("rows"),
        P("rows"),
        P("rows", "rep"),
        P(None, "rep"),
        P("rows", "rep"),
        P("rows", "rep"),
    )
    return jax.shard_map(
        shards,
        mesh=mesh,
        in_specs=placed,
        out_specs=(P(None, "rep"), P("rows", "rep"), P("rows", "rep"), P("rows", "rep"), P("rows")),
        check_vma=False,
    )
```

profile of v0, /device:TPU:0, one launch (start us, length us, event | category | flops | bytes accessed | tf_op | source)
XLA Modules:
  0.0 51.1 jit_solution(4691273592888190196)
XLA Ops:
  0.6 1.0 %shard_map.110.refs_0_ = bf16[288,256]{1,0:T(8,128)(2,1)S(1)} custom-call(bf16[256,256]{1,0:T(8,128)(2,1)} %emb_ref.1, s32[1,256]{1,0:T(1,128)} %bitcast.6, s32[1,256]{1,0:T(1,128)} %bitcast.7, s32[16,256]{1,0:T(8,128)} %bitcast.5), custom_call_target="tpu_custom_call" | custom-call | tf_op jit(solution)/shard_map/pallas_call | solution.py:357
  1.6 5.1 %collective-permute-start.2 = (bf16[288,256]{1,0:T(8,128)(2,1)S(1)}, bf16[288,256]{1,0:T(8,128)(2,1)S(1)}, u32[]{:S(2)}, u32[]{:S(2)}) collective-permute-start(bf16[288,256]{1,0:T(8,128)(2,1)S(1)} %shard_map.110.refs_0_), channel_id=1, source_target_pairs={{0,24},{4,28},{8,0},{12,4},{16,8},{20,12},{24,16},{28,20},{1,25},{... | collective-permute-start | bytes 442376 | tf_op jit(solution)/shard_map/ppermute | solution.py:336
  6.8 0.0 collective-permute-start.1
  6.8 1.0 %collective-permute-start = (bf16[288,256]{1,0:T(8,128)(2,1)S(1)}, bf16[288,256]{1,0:T(8,128)(2,1)S(1)}, u32[]{:S(2)}, u32[]{:S(2)}) collective-permute-start(bf16[288,256]{1,0:T(8,128)(2,1)S(1)} %shard_map.110.refs_0_), channel_id=1, source_target_pairs={{0,8},{4,12},{8,16},{12,20},{16,24},{20,28},{24,0},{28,4},{1,9},{5... | collective-permute-start | bytes 442376 | tf_op jit(solution)/shard_map/ppermute | solution.py:336
  7.8 1.5 %collective-permute-start.3 = (bf16[288,256]{1,0:T(8,128)(2,1)S(1)}, bf16[288,256]{1,0:T(8,128)(2,1)S(1)}, u32[]{:S(2)}, u32[]{:S(2)}) collective-permute-start(bf16[288,256]{1,0:T(8,128)(2,1)S(1)} %shard_map.110.refs_0_), channel_id=1, source_target_pairs={{0,4},{4,0},{8,12},{12,8},{16,20},{20,16},{24,28},{28,24},{1,5},{5... | collective-permute-start | bytes 442376 | tf_op jit(solution)/shard_map/ppermute | solution.py:336
  9.3 1.7 %collective-permute-done.2.refs_3_ = bf16[288,256]{1,0:T(8,128)(2,1)S(1)} collective-permute-done((bf16[288,256]{1,0:T(8,128)(2,1)S(1)}, bf16[288,256]{1,0:T(8,128)(2,1)S(1)}, u32[]{:S(2)}, u32[]{:S(2)}) %collective-permute-start.2) | collective-permute-done | bytes 147488 | tf_op jit(solution)/shard_map/ppermute | solution.py:336
  11.1 1.5 %collective-permute-start.6 = (bf16[288,256]{1,0:T(8,128)(2,1)S(1)}, bf16[288,256]{1,0:T(8,128)(2,1)S(1)}, u32[]{:S(2)}, u32[]{:S(2)}) collective-permute-start(bf16[288,256]{1,0:T(8,128)(2,1)S(1)} %collective-permute-done.2.refs_3_), channel_id=1, source_target_pairs={{0,4},{4,0},{8,12},{12,8},{16,20},{20,16},{24,28},{28,24},{1,5},{5... | collective-permute-start | bytes 442376 | tf_op jit(solution)/shard_map/ppermute | solution.py:336
  12.6 6.7 %collective-permute-done.1.refs_2_ = bf16[288,256]{1,0:T(8,128)(2,1)S(1)} collective-permute-done((bf16[288,256]{1,0:T(8,128)(2,1)S(1)}, bf16[288,256]{1,0:T(8,128)(2,1)S(1)}, u32[]{:S(2)}, u32[]{:S(2)}) %collective-permute-start.1) | collective-permute-done | bytes 147488 | tf_op jit(solution)/shard_map/ppermute | solution.py:336
  19.3 1.5 %collective-permute-start.5 = (bf16[288,256]{1,0:T(8,128)(2,1)S(1)}, bf16[288,256]{1,0:T(8,128)(2,1)S(1)}, u32[]{:S(2)}, u32[]{:S(2)}) collective-permute-start(bf16[288,256]{1,0:T(8,128)(2,1)S(1)} %collective-permute-done.1.refs_2_), channel_id=1, source_target_pairs={{0,4},{4,0},{8,12},{12,8},{16,20},{20,16},{24,28},{28,24},{1,5},{5... | collective-permute-start | bytes 442376 | tf_op jit(solution)/shard_map/ppermute | solution.py:336
  20.8 0.0 collective-permute-done.refs_1_
  20.8 0.5 collective-permute-start.4
  21.3 1.0 %shard_map.111 = (f32[256,256]{1,0:T(8,128)S(1)}, f32[32,256]{1,0:T(8,128)S(1)}) custom-call(f32[256,256]{1,0:T(8,128)} %coarse_ref.1, f32[32,256]{1,0:T(8,128)} %book_ref.1), custom_call_target="tpu_custom_call" | custom-call | flops 1000000 | bytes 1000000 | tf_op jit(solution)/shard_map/pallas_call | solution.py:363
  22.3 0.0 collective-permute-done.3.refs_4_
  22.3 0.0 collective-permute-done.6.refs_7_
  22.3 3.7 %collective-permute-done.5.refs_6_ = bf16[288,256]{1,0:T(8,128)(2,1)S(1)} collective-permute-done((bf16[288,256]{1,0:T(8,128)(2,1)S(1)}, bf16[288,256]{1,0:T(8,128)(2,1)S(1)}, u32[]{:S(2)}, u32[]{:S(2)}) %collective-permute-start.5) | collective-permute-done | bytes 147488 | tf_op jit(solution)/shard_map/ppermute | solution.py:336
  26.0 1.6 %collective-permute-done.4.refs_5_ = bf16[288,256]{1,0:T(8,128)(2,1)S(1)} collective-permute-done((bf16[288,256]{1,0:T(8,128)(2,1)S(1)}, bf16[288,256]{1,0:T(8,128)(2,1)S(1)}, u32[]{:S(2)}, u32[]{:S(2)}) %collective-permute-start.4) | collective-permute-done | bytes 147488 | tf_op jit(solution)/shard_map/ppermute | solution.py:336
  27.6 17.8 %shard_map.112 = (f32[256,256]{1,0:T(8,128)}, f32[8192,256]{1,0:T(8,128)}, bf16[256,256]{1,0:T(8,128)(2,1)}, f32[32,256]{1,0:T(8,128)}, f32[1,256]{1,0:T(1,128)S(1)}) custom-call(bf16[288,256]{1,0:T(8,128)(2,1)S(1)} %shard_map.110.refs_0_, bf16[288,256]{1,0:T(8,128)(2,1)S(1)} %collective-permute-done.refs_1_, ...), custom_call_target="tpu_custom_call" | custom-call | tf_op jit(solution)/shard_map/pallas_call | solution.py:370
  45.4 5.1 %all-gather = f32[4,1,256]{2,1,0:T(1,128)S(1)} all-gather(f32[1,1,256]{2,1,0:T(1,128)S(1)} %bitcast.4), channel_id=1, replica_groups=mesh['rows'=8,'rep'=4] {'rep'}, dimensions={0}, use_global_device_ids=true | all-gather | bytes 5120 | tf_op jit(solution)/shard_map/all_gather | solution.py:396
  50.5 0.6 %broadcast_multiply_fusion = f32[256]{0:T(256)} fusion(f32[256]{0:T(256)S(1)} %reduce_sum.9), kind=kLoop, calls=%fused_computation | loop fusion | flops 256 | bytes 2048 | tf_op jit(solution)/shard_map/div | solution.py:396
  (1 shorter events, 0.0 us)
Async XLA Ops:
  1.6 9.4 %collective-permute-start.2 = (bf16[288,256]{1,0:T(8,128)(2,1)S(1)}, bf16[288,256]{1,0:T(8,128)(2,1)S(1)}, u32[]{:S(2)}, u32[]{:S(2)}) collective-permute-start(bf16[288,256]{1,0:T(8,128)(2,1)S(1)} %shard_map.110.refs_0_), channel_id=1, source_target_pairs={{0,24},{4,28},{8,0},{12,4},{16,8},{20,12},{24,16},{28,20},{1,25},{... | collective-permute-start | bytes 442376 | tf_op jit(solution)/shard_map/ppermute | solution.py:336
  6.8 12.5 %collective-permute-start.1 = (bf16[288,256]{1,0:T(8,128)(2,1)S(1)}, bf16[288,256]{1,0:T(8,128)(2,1)S(1)}, u32[]{:S(2)}, u32[]{:S(2)}) collective-permute-start(bf16[288,256]{1,0:T(8,128)(2,1)S(1)} %shard_map.110.refs_0_), channel_id=1, source_target_pairs={{0,16},{4,20},{8,24},{12,28},{16,0},{20,4},{24,8},{28,12},{1,17},{... | collective-permute-start | bytes 442376 | tf_op jit(solution)/shard_map/ppermute | solution.py:336
  6.8 14.0 %collective-permute-start = (bf16[288,256]{1,0:T(8,128)(2,1)S(1)}, bf16[288,256]{1,0:T(8,128)(2,1)S(1)}, u32[]{:S(2)}, u32[]{:S(2)}) collective-permute-start(bf16[288,256]{1,0:T(8,128)(2,1)S(1)} %shard_map.110.refs_0_), channel_id=1, source_target_pairs={{0,8},{4,12},{8,16},{12,20},{16,24},{20,28},{24,0},{28,4},{1,9},{5... | collective-permute-start | bytes 442376 | tf_op jit(solution)/shard_map/ppermute | solution.py:336
  7.8 14.5 %collective-permute-start.3 = (bf16[288,256]{1,0:T(8,128)(2,1)S(1)}, bf16[288,256]{1,0:T(8,128)(2,1)S(1)}, u32[]{:S(2)}, u32[]{:S(2)}) collective-permute-start(bf16[288,256]{1,0:T(8,128)(2,1)S(1)} %shard_map.110.refs_0_), channel_id=1, source_target_pairs={{0,4},{4,0},{8,12},{12,8},{16,20},{20,16},{24,28},{28,24},{1,5},{5... | collective-permute-start | bytes 442376 | tf_op jit(solution)/shard_map/ppermute | solution.py:336
  11.1 11.2 %collective-permute-start.6 = (bf16[288,256]{1,0:T(8,128)(2,1)S(1)}, bf16[288,256]{1,0:T(8,128)(2,1)S(1)}, u32[]{:S(2)}, u32[]{:S(2)}) collective-permute-start(bf16[288,256]{1,0:T(8,128)(2,1)S(1)} %collective-permute-done.2.refs_3_), channel_id=1, source_target_pairs={{0,4},{4,0},{8,12},{12,8},{16,20},{20,16},{24,28},{28,24},{1,5},{5... | collective-permute-start | bytes 442376 | tf_op jit(solution)/shard_map/ppermute | solution.py:336
  19.3 6.7 %collective-permute-start.5 = (bf16[288,256]{1,0:T(8,128)(2,1)S(1)}, bf16[288,256]{1,0:T(8,128)(2,1)S(1)}, u32[]{:S(2)}, u32[]{:S(2)}) collective-permute-start(bf16[288,256]{1,0:T(8,128)(2,1)S(1)} %collective-permute-done.1.refs_2_), channel_id=1, source_target_pairs={{0,4},{4,0},{8,12},{12,8},{16,20},{20,16},{24,28},{28,24},{1,5},{5... | collective-permute-start | bytes 442376 | tf_op jit(solution)/shard_map/ppermute | solution.py:336
  20.8 6.8 %collective-permute-start.4 = (bf16[288,256]{1,0:T(8,128)(2,1)S(1)}, bf16[288,256]{1,0:T(8,128)(2,1)S(1)}, u32[]{:S(2)}, u32[]{:S(2)}) collective-permute-start(bf16[288,256]{1,0:T(8,128)(2,1)S(1)} %collective-permute-done.refs_1_), channel_id=1, source_target_pairs={{0,4},{4,0},{8,12},{12,8},{16,20},{20,16},{24,28},{28,24},{1,5},{5... | collective-permute-start | bytes 442376 | tf_op jit(solution)/shard_map/ppermute | solution.py:336
where the time goes:
time: 50.8 us; the launch traced here: 51.1 us
  Pallas kernels  19.8 us (39%)
  waiting for transfers between devices  13.8 us (27%)
  starting transfers between devices  11.2 us (22%)
  blocking collectives  5.07 us (10%)
  between operations  0.67 us (1%)
  other arithmetic  0.59 us (1%)
    pallas_call x1, Pallas kernels, gathered_shards(): pl.pallas_call(functools.partial(steps_kernel, blocks), out_shape=(jax.Sh...  17.8 us
    ppermute x7, waiting for transfers between devices, hop(): return lax.ppermute(value, 'rows', pairs)  13.8 us
    ppermute x7, starting transfers between devices, hop(): return lax.ppermute(value, 'rows', pairs)  11.2 us
    all_gather x1, blocking collectives, gathered_shards(): lax.all_gather(error, 'rep', axis=0, tiled=True)  5.07 us
  transfers between devices with their start and end apart: 7, of which 4 were waited for; matrix products, arithmetic and copies ran while one was open for 0% of the time, Pallas kernels for 2%

commit v1 on v0

--- a/solution.py
+++ b/solution.py
@@ -332,15 +332,20 @@
 
 
 def gather_blocks(block, count):
-    def hop(value, pairs):
-        return lax.ppermute(value, "rows", pairs)
-
-    half = count // 2
-    near = [block]
-    for k in range(1, half):
-        near.append(hop(block, [(i, (i + 2 * k) % count) for i in range(count)]))
-    far = [hop(value, [(i, i ^ 1) for i in range(count)]) for value in near]
-    return near + far
+    def flip(value, step):
+        return lax.ppermute(value, "rows", [(i, i ^ step) for i in range(count)])
+
+    near = {0: block}
+    step = count // 2
+    while step > 1:
+        near.update({at + step: flip(value, step) for at, value in list(near.items())})
+        step //= 2
+    last, top = count - 2, count // 2
+    far = {at: flip(value, 1) for at, value in near.items() if at != last or count < 4}
+    if count >= 4:
+        far[last] = flip(far[last - top], top)
+    order = sorted(near)
+    return [near[at] for at in order] + [far[at] for at in order]
 
 
 def gathered_shards(embeddings, coarse_ids, fine_ids, pq_codes, old_coarse, old_fine, old_codebook):
@@ -401,7 +406,8 @@
     rows, width, blocks, fine_dev, sub_dev, code_total, coarse_total, fine_total = sizes
     digits = 256
     return (
-        blocks % 2 == 0
+        blocks > 1
+        and blocks & (blocks - 1) == 0
         and rows * blocks <= fine_dev
         and rows % 128 == 0
         and rows <= digits

time: 50.8 us -> 45.6 us (0.90)
  waiting for transfers between devices: 13.8 us -> 10 us
  Pallas kernels: 19.8 us -> 17.1 us
  starting transfers between devices: 11.2 us -> 12.1 us
    ppermute x7, waiting for transfers between devices: 13.8 us -> 10 us  [flip(): return lax.ppermute(value, 'rows', [(i, i ^ step) for i in range(count)])]
    pallas_call x1, Pallas kernels: 17.8 us -> 15.2 us  [gathered_shards(): pl.pallas_call(functools.partial(steps_kernel, blocks), out_shape=(jax.Sh...]
    ppermute x7, starting transfers between devices: 11.2 us -> 12.1 us  [flip(): return lax.ppermute(value, 'rows', [(i, i ^ step) for i in range(count)])]
  transfers between devices with their start and end apart: 7 -> 7, of which waited for: 4 -> 5; matrix products, arithmetic and copies ran while one was open for 0% -> 0% of each run, Pallas kernels for 2% -> 2%
where the time goes in v1:
time: 45.6 us
  Pallas kernels  17.1 us (38%)
  starting transfers between devices  12.1 us (27%)
  waiting for transfers between devices  10 us (22%)
  blocking collectives  5.07 us (11%)
  between operations  0.67 us (1%)
  other arithmetic  0.59 us (1%)
    pallas_call x1, Pallas kernels, gathered_shards(): pl.pallas_call(functools.partial(steps_kernel, blocks), out_shape=(jax.Sh...  15.2 us
    ppermute x7, starting transfers between devices, flip(): return lax.ppermute(value, 'rows', [(i, i ^ step) for i in range(count)])  12.1 us
    ppermute x7, waiting for transfers between devices, flip(): return lax.ppermute(value, 'rows', [(i, i ^ step) for i in range(count)])  10 us
    all_gather x1, blocking collectives, gathered_shards(): lax.all_gather(error, 'rep', axis=0, tiled=True)  5.07 us
    pallas_call x1, Pallas kernels, gathered_shards(): pl.pallas_call(pack_kernel, out_shape=pltpu.VMEM((height, rows), jnp.bflo...  1.01 us
    pallas_call x1, Pallas kernels, gathered_shards(): pl.pallas_call(stage_kernel, out_shape=(pltpu.VMEM(old_coarse.shape, jnp....  0.97 us
  transfers between devices with their start and end apart: 7, of which 5 were waited for; matrix products, arithmetic and copies ran while one was open for 0% of the time, Pallas kernels for 2%

profile of v1, /device:TPU:0, one launch (start us, length us, event | category | flops | bytes accessed | tf_op | source)
XLA Modules:
  0.0 45.6 jit_solution(1898945682726996760)
XLA Ops:
  0.6 1.0 %shard_map.110.refs_0_ = bf16[288,256]{1,0:T(8,128)(2,1)S(1)} custom-call(bf16[256,256]{1,0:T(8,128)(2,1)} %emb_ref.1, s32[1,256]{1,0:T(1,128)} %bitcast.6, s32[1,256]{1,0:T(1,128)} %bitcast.7, s32[16,256]{1,0:T(8,128)} %bitcast.5), custom_call_target="tpu_custom_call" | custom-call | tf_op jit(solution)/shard_map/pallas_call | solution.py:362
  1.6 3.1 %collective-permute-start = (bf16[288,256]{1,0:T(8,128)(2,1)S(1)}, bf16[288,256]{1,0:T(8,128)(2,1)S(1)}, u32[]{:S(2)}, u32[]{:S(2)}) collective-permute-start(bf16[288,256]{1,0:T(8,128)(2,1)S(1)} %shard_map.110.refs_0_), channel_id=1, source_target_pairs={{0,8},{4,12},{8,0},{12,4},{16,24},{20,28},{24,16},{28,20},{1,9},{5... | collective-permute-start | bytes 442376 | tf_op jit(solution)/shard_map/ppermute | solution.py:336
  4.8 2.6 %collective-permute-start.1 = (bf16[288,256]{1,0:T(8,128)(2,1)S(1)}, bf16[288,256]{1,0:T(8,128)(2,1)S(1)}, u32[]{:S(2)}, u32[]{:S(2)}) collective-permute-start(bf16[288,256]{1,0:T(8,128)(2,1)S(1)} %shard_map.110.refs_0_), channel_id=1, source_target_pairs={{0,16},{4,20},{8,24},{12,28},{16,0},{20,4},{24,8},{28,12},{1,17},{... | collective-permute-start | bytes 442376 | tf_op jit(solution)/shard_map/ppermute | solution.py:336
  7.4 3.8 %collective-permute-done.refs_1_ = bf16[288,256]{1,0:T(8,128)(2,1)S(1)} collective-permute-done((bf16[288,256]{1,0:T(8,128)(2,1)S(1)}, bf16[288,256]{1,0:T(8,128)(2,1)S(1)}, u32[]{:S(2)}, u32[]{:S(2)}) %collective-permute-start) | collective-permute-done | bytes 147488 | tf_op jit(solution)/shard_map/ppermute | solution.py:336
  11.2 1.8 %collective-permute-start.4 = (bf16[288,256]{1,0:T(8,128)(2,1)S(1)}, bf16[288,256]{1,0:T(8,128)(2,1)S(1)}, u32[]{:S(2)}, u32[]{:S(2)}) collective-permute-start(bf16[288,256]{1,0:T(8,128)(2,1)S(1)} %collective-permute-done.refs_1_), channel_id=1, source_target_pairs={{0,4},{4,0},{8,12},{12,8},{16,20},{20,16},{24,28},{28,24},{1,5},{5... | collective-permute-start | bytes 442376 | tf_op jit(solution)/shard_map/ppermute | solution.py:336
  13.0 0.2 collective-permute-start.3
  13.2 1.0 %collective-permute-done.1.refs_2_ = bf16[288,256]{1,0:T(8,128)(2,1)S(1)} collective-permute-done((bf16[288,256]{1,0:T(8,128)(2,1)S(1)}, bf16[288,256]{1,0:T(8,128)(2,1)S(1)}, u32[]{:S(2)}, u32[]{:S(2)}) %collective-permute-start.1) | collective-permute-done | bytes 147488 | tf_op jit(solution)/shard_map/ppermute | solution.py:336
  14.2 1.5 %collective-permute-start.5 = (bf16[288,256]{1,0:T(8,128)(2,1)S(1)}, bf16[288,256]{1,0:T(8,128)(2,1)S(1)}, u32[]{:S(2)}, u32[]{:S(2)}) collective-permute-start(bf16[288,256]{1,0:T(8,128)(2,1)S(1)} %collective-permute-done.1.refs_2_), channel_id=1, source_target_pairs={{0,4},{4,0},{8,12},{12,8},{16,20},{20,16},{24,28},{28,24},{1,5},{5... | collective-permute-start | bytes 442376 | tf_op jit(solution)/shard_map/ppermute | solution.py:336
  15.7 0.4 collective-permute-start.2
  16.2 0.6 %collective-permute-done.4.refs_5_ = bf16[288,256]{1,0:T(8,128)(2,1)S(1)} collective-permute-done((bf16[288,256]{1,0:T(8,128)(2,1)S(1)}, bf16[288,256]{1,0:T(8,128)(2,1)S(1)}, u32[]{:S(2)}, u32[]{:S(2)}) %collective-permute-start.4) | collective-permute-done | bytes 147488 | tf_op jit(solution)/shard_map/ppermute | solution.py:336
  16.8 2.4 %collective-permute-start.6 = (bf16[288,256]{1,0:T(8,128)(2,1)S(1)}, bf16[288,256]{1,0:T(8,128)(2,1)S(1)}, u32[]{:S(2)}, u32[]{:S(2)}) collective-permute-start(bf16[288,256]{1,0:T(8,128)(2,1)S(1)} %collective-permute-done.4.refs_5_), channel_id=1, source_target_pairs={{0,16},{4,20},{8,24},{12,28},{16,0},{20,4},{24,8},{28,12},{1,17},{... | collective-permute-start | bytes 442376 | tf_op jit(solution)/shard_map/ppermute | solution.py:336
  19.2 1.0 %shard_map.111 = (f32[256,256]{1,0:T(8,128)S(1)}, f32[32,256]{1,0:T(8,128)S(1)}) custom-call(f32[256,256]{1,0:T(8,128)} %coarse_ref.1, f32[32,256]{1,0:T(8,128)} %book_ref.1), custom_call_target="tpu_custom_call" | custom-call | flops 1000000 | bytes 1000000 | tf_op jit(solution)/shard_map/pallas_call | solution.py:368
  20.2 0.0 collective-permute-done.3.refs_4_
  20.2 0.0 collective-permute-done.5.refs_6_
  20.2 0.9 %collective-permute-done.2.refs_3_ = bf16[288,256]{1,0:T(8,128)(2,1)S(1)} collective-permute-done((bf16[288,256]{1,0:T(8,128)(2,1)S(1)}, bf16[288,256]{1,0:T(8,128)(2,1)S(1)}, u32[]{:S(2)}, u32[]{:S(2)}) %collective-permute-start.2) | collective-permute-done | bytes 147488 | tf_op jit(solution)/shard_map/ppermute | solution.py:336
  21.1 3.6 %collective-permute-done.6.refs_7_ = bf16[288,256]{1,0:T(8,128)(2,1)S(1)} collective-permute-done((bf16[288,256]{1,0:T(8,128)(2,1)S(1)}, bf16[288,256]{1,0:T(8,128)(2,1)S(1)}, u32[]{:S(2)}, u32[]{:S(2)}) %collective-permute-start.6) | collective-permute-done | bytes 147488 | tf_op jit(solution)/shard_map/ppermute | solution.py:336
  24.8 15.2 %shard_map.112 = (f32[256,256]{1,0:T(8,128)}, f32[8192,256]{1,0:T(8,128)}, bf16[256,256]{1,0:T(8,128)(2,1)}, f32[32,256]{1,0:T(8,128)}, f32[1,256]{1,0:T(1,128)S(1)}) custom-call(bf16[288,256]{1,0:T(8,128)(2,1)S(1)} %shard_map.110.refs_0_, bf16[288,256]{1,0:T(8,128)(2,1)S(1)} %collective-permute-done.refs_1_, ...), custom_call_target="tpu_custom_call" | custom-call | tf_op jit(solution)/shard_map/pallas_call | solution.py:375
  39.9 5.1 %all-gather = f32[4,1,256]{2,1,0:T(1,128)S(1)} all-gather(f32[1,1,256]{2,1,0:T(1,128)S(1)} %bitcast.4), channel_id=1, replica_groups=mesh['rows'=8,'rep'=4] {'rep'}, dimensions={0}, use_global_device_ids=true | all-gather | bytes 5120 | tf_op jit(solution)/shard_map/all_gather | solution.py:401
  45.0 0.6 %broadcast_multiply_fusion = f32[256]{0:T(256)} fusion(f32[256]{0:T(256)S(1)} %reduce_sum.9), kind=kLoop, calls=%fused_computation | loop fusion | flops 256 | bytes 2048 | tf_op jit(solution)/shard_map/div | solution.py:401
  (1 shorter events, 0.0 us)
Async XLA Ops:
  1.6 9.5 %collective-permute-start = (bf16[288,256]{1,0:T(8,128)(2,1)S(1)}, bf16[288,256]{1,0:T(8,128)(2,1)S(1)}, u32[]{:S(2)}, u32[]{:S(2)}) collective-permute-start(bf16[288,256]{1,0:T(8,128)(2,1)S(1)} %shard_map.110.refs_0_), channel_id=1, source_target_pairs={{0,8},{4,12},{8,0},{12,4},{16,24},{20,28},{24,16},{28,20},{1,9},{5... | collective-permute-start | bytes 442376 | tf_op jit(solution)/shard_map/ppermute | solution.py:336
  4.8 9.4 %collective-permute-start.1 = (bf16[288,256]{1,0:T(8,128)(2,1)S(1)}, bf16[288,256]{1,0:T(8,128)(2,1)S(1)}, u32[]{:S(2)}, u32[]{:S(2)}) collective-permute-start(bf16[288,256]{1,0:T(8,128)(2,1)S(1)} %shard_map.110.refs_0_), channel_id=1, source_target_pairs={{0,16},{4,20},{8,24},{12,28},{16,0},{20,4},{24,8},{28,12},{1,17},{... | collective-permute-start | bytes 442376 | tf_op jit(solution)/shard_map/ppermute | solution.py:336
  11.2 5.6 %collective-permute-start.4 = (bf16[288,256]{1,0:T(8,128)(2,1)S(1)}, bf16[288,256]{1,0:T(8,128)(2,1)S(1)}, u32[]{:S(2)}, u32[]{:S(2)}) collective-permute-start(bf16[288,256]{1,0:T(8,128)(2,1)S(1)} %collective-permute-done.refs_1_), channel_id=1, source_target_pairs={{0,4},{4,0},{8,12},{12,8},{16,20},{20,16},{24,28},{28,24},{1,5},{5... | collective-permute-start | bytes 442376 | tf_op jit(solution)/shard_map/ppermute | solution.py:336
  13.0 7.2 %collective-permute-start.3 = (bf16[288,256]{1,0:T(8,128)(2,1)S(1)}, bf16[288,256]{1,0:T(8,128)(2,1)S(1)}, u32[]{:S(2)}, u32[]{:S(2)}) collective-permute-start(bf16[288,256]{1,0:T(8,128)(2,1)S(1)} %shard_map.110.refs_0_), channel_id=1, source_target_pairs={{0,4},{4,0},{8,12},{12,8},{16,20},{20,16},{24,28},{28,24},{1,5},{5... | collective-permute-start | bytes 442376 | tf_op jit(solution)/shard_map/ppermute | solution.py:336
  14.2 6.0 %collective-permute-start.5 = (bf16[288,256]{1,0:T(8,128)(2,1)S(1)}, bf16[288,256]{1,0:T(8,128)(2,1)S(1)}, u32[]{:S(2)}, u32[]{:S(2)}) collective-permute-start(bf16[288,256]{1,0:T(8,128)(2,1)S(1)} %collective-permute-done.1.refs_2_), channel_id=1, source_target_pairs={{0,4},{4,0},{8,12},{12,8},{16,20},{20,16},{24,28},{28,24},{1,5},{5... | collective-permute-start | bytes 442376 | tf_op jit(solution)/shard_map/ppermute | solution.py:336
  15.7 5.4 %collective-permute-start.2 = (bf16[288,256]{1,0:T(8,128)(2,1)S(1)}, bf16[288,256]{1,0:T(8,128)(2,1)S(1)}, u32[]{:S(2)}, u32[]{:S(2)}) collective-permute-start(bf16[288,256]{1,0:T(8,128)(2,1)S(1)} %collective-permute-done.1.refs_2_), channel_id=1, source_target_pairs={{0,8},{4,12},{8,0},{12,4},{16,24},{20,28},{24,16},{28,20},{1,9},{5... | collective-permute-start | bytes 442376 | tf_op jit(solution)/shard_map/ppermute | solution.py:336
  16.8 8.0 %collective-permute-start.6 = (bf16[288,256]{1,0:T(8,128)(2,1)S(1)}, bf16[288,256]{1,0:T(8,128)(2,1)S(1)}, u32[]{:S(2)}, u32[]{:S(2)}) collective-permute-start(bf16[288,256]{1,0:T(8,128)(2,1)S(1)} %collective-permute-done.4.refs_5_), channel_id=1, source_target_pairs={{0,16},{4,20},{8,24},{12,28},{16,0},{20,4},{24,8},{28,12},{1,17},{... | collective-permute-start | bytes 442376 | tf_op jit(solution)/shard_map/ppermute | solution.py:336
